TPU v7x, 32 devices: a whole 2x2x4 slice. The times are simulated.
32 devices in a mesh: row: 4 (over x, core), col: 8 (over z, y).
Axes of the slice: x: 2, y: 2, z: 4, core: 2. Of those that a mesh axis runs over, the one named last changes fastest.
Arguments:
- rhs: float32 [4, 8, 8, 4, 128], P('row', 'col'), may hold values from -6 to 6
- diag0: float32 [4, 8, 8, 128], P('row', 'col'), may hold values from 2 to 4
- blocks0: float32 [4, 8, 8, 14, 128, 128], P('row', 'col'), may hold values from -0.1875 to 0.1875
- cols0: int32 [4, 8, 8, 14], P('row', 'col'), may hold values from 0 to 23
- sends0: int32 [4, 8, 4, 4], P('row', 'col'), may hold values from 0 to 7
- pro0: float32 [4, 8, 8, 128, 128], P('row', 'col'), may hold values from -0.5 to 0.5
- agg0: int32 [4, 8, 8], P('row', 'col'), may hold values from 0 to 1
- diag1: float32 [4, 8, 2, 128], P('row', 'col'), may hold values from 2 to 4
- blocks1: float32 [4, 8, 2, 14, 128, 128], P('row', 'col'), may hold values from -0.1875 to 0.1875
- cols1: int32 [4, 8, 2, 14], P('row', 'col'), may hold values from 0 to 9
- sends1: int32 [4, 8, 4, 2], P('row', 'col'), may hold values from 0 to 1
- pro1: float32 [4, 8, 2, 128, 128], P('row', 'col'), may hold values from -0.25 to 0.25
- agg1: int32 [4, 8, 2], P('row', 'col'), may hold values from 0 to 7
- cinv: float32 [1024, 1024], P(('row', 'col')), may hold values from -0.1875 to 0.1875
Outputs:
- solution: float32 [4, 8, 8, 4, 128], P('row', 'col')
Inputs may be any that keep to these rules, and one draw needn't show every extreme that they name: `sends0`: indices of the sender's own fine blocks. `sends1`: indices of the sender's own level-one blocks. `cols0`: indices into the extended fine vector of 24 blocks. `cols1`: indices into the extended level-one vector of 10 blocks. `agg0`: a level-one block of the same partition. `agg1`: a coarsest block, on any partition.
All inputs are finite; a program needn't handle non-finite values.
Results may differ from a plain program's by a relative error of at most 0.0001.
Values sent between devices are 32-bit elements; how exact they have to be, the bound alone decides.
No kernel may reach another device: no remote copies, remote signals or barrier semaphores. Data moves between devices by JAX's collectives and lax.ppermute only.
A program may use at most 64 MiB of HBM per device.

v0:
```python
import jax
import jax.numpy as jnp
from jax import lax
from jax.sharding import PartitionSpec as P

NU = 2
HIGH = lax.Precision.HIGHEST
OMEGA = 0.3


def padded_2(value, sides, width):
    for axis, dim in sides:
        size, length = (lax.axis_size(axis), value.shape[dim])
        up = [(i, (i + 1) % size) for i in range(size - 1)]
        down = [(j, i) for i, j in up]
        last = lax.slice_in_dim(value, length - width, length, axis=dim)
        leading = lax.slice_in_dim(value, 0, width, axis=dim)
        before = lax.ppermute(last, axis, up)
        after = lax.ppermute(leading, axis, down)
        value = jnp.concatenate([before, value, after], axis=dim)
    return value


def gather_ghosts(vector, sends):
    packed = vector[sends]
    padded = padded_2(packed[None, None], (("row", 0), ("col", 1)), 1)
    return jnp.concatenate(
        [vector, padded[0, 1, 0], padded[2, 1, 1], padded[1, 0, 2], padded[1, 2, 3]], axis=0
    )


def apply_op(vector, diag, blocks, cols, sends):
    extended = gather_ghosts(vector, sends)
    nearby = extended[cols]
    coupled = jnp.einsum("bkij,bkrj->bri", blocks, nearby, precision=HIGH)
    return diag[:, None, :] * vector + coupled


def smooth(vector, right_side, diag, blocks, cols, sends, count):
    for sweep in range(count):
        vector = (
            vector
            + OMEGA * (right_side - apply_op(vector, diag, blocks, cols, sends)) / diag[:, None, :]
        )
    return vector


def on_device(
    rhs, diag0, blocks0, cols0, sends0, pro0, agg0, diag1, blocks1, cols1, sends1, pro1, agg1, cinv
):
    fine_rhs = rhs[0, 0]
    fine_diag = diag0[0, 0]
    fine_blocks = blocks0[0, 0]
    fine_cols = cols0[0, 0]
    fine_sends = sends0[0, 0]
    fine_pro = pro0[0, 0]
    level_diag = diag1[0, 0]
    level_blocks = blocks1[0, 0]
    level_cols = cols1[0, 0]
    level_sends = sends1[0, 0]
    level_pro = pro1[0, 0]
    level_count = level_diag.shape[0]
    block_size = level_diag.shape[1]
    loads = fine_rhs.shape[1]
    coarse_total = cinv.shape[1]
    coarse_count = coarse_total // block_size
    fine_x = OMEGA * fine_rhs / fine_diag[:, None, :]
    fine_x = smooth(fine_x, fine_rhs, fine_diag, fine_blocks, fine_cols, fine_sends, NU - 1)
    fine_res = fine_rhs - apply_op(fine_x, fine_diag, fine_blocks, fine_cols, fine_sends)
    onehot0 = (agg0[0, 0][:, None] == jnp.arange(level_count)).astype(jnp.float32)
    restricted = jnp.einsum("bij,bri->brj", fine_pro, fine_res, precision=HIGH)
    level_rhs = jnp.einsum("bc,brj->crj", onehot0, restricted, precision=HIGH)
    level_x = OMEGA * level_rhs / level_diag[:, None, :]
    level_x = smooth(level_x, level_rhs, level_diag, level_blocks, level_cols, level_sends, NU - 1)
    level_res = level_rhs - apply_op(level_x, level_diag, level_blocks, level_cols, level_sends)
    onehot1 = (agg1[0, 0][:, None] == jnp.arange(coarse_count)).astype(jnp.float32)
    contrib = jnp.einsum("bij,bri->brj", level_pro, level_res, precision=HIGH)
    term = jnp.einsum("bc,brj->rcj", onehot1, contrib, precision=HIGH).reshape(loads, coarse_total)
    coarse_rhs = lax.psum(term, ("row", "col"))
    own_rows = jnp.einsum("ij,rj->ri", cinv, coarse_rhs, precision=HIGH)
    coarse_x = lax.all_gather(own_rows, ("row", "col"), axis=1, tiled=True)
    coarse_blocks = coarse_x.reshape(loads, coarse_count, block_size)
    picked = jnp.einsum("bc,rcj->brj", onehot1, coarse_blocks, precision=HIGH)
    level_x = level_x + jnp.einsum("bij,brj->bri", level_pro, picked, precision=HIGH)
    level_x = smooth(level_x, level_rhs, level_diag, level_blocks, level_cols, level_sends, NU)
    lifted = jnp.einsum("bc,crj->brj", onehot0, level_x, precision=HIGH)
    fine_x = fine_x + jnp.einsum("bij,brj->bri", fine_pro, lifted, precision=HIGH)
    fine_x = smooth(fine_x, fine_rhs, fine_diag, fine_blocks, fine_cols, fine_sends, NU)
    return fine_x[None, None]


def solution(mesh):
    return jax.shard_map(
        on_device,
        mesh=mesh,
        in_specs=(
            P("row", "col", None, None, None),
            P("row", "col", None, None),
            P("row", "col", None, None, None, None),
            P("row", "col", None, None),
            P("row", "col", None, None),
            P("row", "col", None, None, None),
            P("row", "col", None),
            P("row", "col", None, None),
            P("row", "col", None, None, None, None),
            P("row", "col", None, None),
            P("row", "col", None, None),
            P("row", "col", None, None, None),
            P("row", "col", None),
            P(("row", "col"), None),
        ),
        out_specs=P("row", "col", None, None, None),
        check_vma=False,
    )
```

profile of v0, /device:TPU:1, one launch (start us, length us, event | category | flops | bytes accessed | tf_op | source)
XLA Modules:
  0.0 297.1 jit_solution(16686773013737030327)
XLA Ops:
  3.1 4.5 %collective-permute-start = (f32[1,1,4,4,4,128]{5,4,3,2,1,0:T(4,128)S(1)}, f32[1,1,4,4,4,128]{5,4,3,2,1,0:T(4,128)S(1)}, u32[]{:S(2)}, u32[]{:S(2)}) collective-permute-start(f32[1,1,4,4,4,128]{5,4,3,2,1,0:T(4,128)S(1)} %bitcast.453), channel_id=1, source_target_pairs={{0,8},{8,16},{16,24},{1,9},{9,17},{17,25},{2,10},{10,18},{18,26},{... | collective-permute-start | bytes 98312 | tf_op jit(solution)/shard_map/ppermute | solution.py:18
  12.9 3.1 %collective-permute-start.2 = (f32[3,1,4,4,4,128]{5,4,3,2,1,0:T(4,128)S(1)}, f32[3,1,4,4,4,128]{5,4,3,2,1,0:T(4,128)S(1)}, u32[]{:S(2)}, u32[]{:S(2)}) collective-permute-start(f32[3,1,4,4,4,128]{5,4,3,2,1,0:T(4,128)S(1)} %pad_maximum_fusion), channel_id=1, source_target_pairs={{0,1},{1,2},{2,3},{3,4},{4,5},{5,6},{6,7},{8,9},{9,10},{10,11},{11... | collective-permute-start | bytes 294920 | tf_op jit(solution)/shard_map/ppermute | solution.py:18
  17.7 3.7 %collective-permute-done.3 = f32[3,1,4,4,4,128]{5,4,3,2,1,0:T(4,128)S(1)} collective-permute-done((f32[3,1,4,4,4,128]{5,4,3,2,1,0:T(4,128)S(1)}, f32[3,1,4,4,4,128]{5,4,3,2,1,0:T(4,128)S(1)}, u32[]{:S(2)}, u32[]{:S(2)}) %collective-permute-start.3) | collective-permute-done | bytes 98336 | tf_op jit(solution)/shard_map/ppermute | solution.py:19
  22.2 8.3 %constant_dynamic-update-slice_fusion.9 = (f32[24,4,128]{2,1,0:T(4,128)S(1)}, f32[8,4,128]{2,1,0:T(4,128)S(1)}) fusion(f32[8,14,4,128]{3,2,1,0:T(4,128)S(1)} %bitcast.438, f32[1,1,8,14,128,128]{5,4,3,2,1,0:T(8,128)} %param.16, f32[8,128]{1,0:T(8,128)} %bitcast.466, f32[1,1,8,4,128]{4,3,2,1,0:T(4,128)} %param.14), kind=kOutput, calls=%fused_computation.94 | convolution fusion | flops 88113152 | bytes 7622656 | tf_op jit(solution)/shard_map/bkij,bkrj->bri/dot_general | solution.py:35
  31.1 3.3 %collective-permute-start.4 = (f32[1,1,4,4,4,128]{5,4,3,2,1,0:T(4,128)S(1)}, f32[1,1,4,4,4,128]{5,4,3,2,1,0:T(4,128)S(1)}, u32[]{:S(2)}, u32[]{:S(2)}) collective-permute-start(f32[1,1,4,4,4,128]{5,4,3,2,1,0:T(4,128)S(1)} %bitcast.456), channel_id=1, source_target_pairs={{0,8},{8,16},{16,24},{1,9},{9,17},{17,25},{2,10},{10,18},{18,26},{... | collective-permute-start | bytes 98312 | tf_op jit(solution)/shard_map/ppermute | solution.py:18
  36.5 3.2 %collective-permute-done.5 = f32[1,1,4,4,4,128]{5,4,3,2,1,0:T(4,128)S(1)} collective-permute-done((f32[1,1,4,4,4,128]{5,4,3,2,1,0:T(4,128)S(1)}, f32[1,1,4,4,4,128]{5,4,3,2,1,0:T(4,128)S(1)}, u32[]{:S(2)}, u32[]{:S(2)}) %collective-permute-start.5) | collective-permute-done | bytes 32800 | tf_op jit(solution)/shard_map/ppermute | solution.py:19
  39.7 4.0 %collective-permute-start.6 = (f32[3,1,4,4,4,128]{5,4,3,2,1,0:T(4,128)S(1)}, f32[3,1,4,4,4,128]{5,4,3,2,1,0:T(4,128)S(1)}, u32[]{:S(2)}, u32[]{:S(2)}) collective-permute-start(f32[3,1,4,4,4,128]{5,4,3,2,1,0:T(4,128)S(1)} %pad_maximum_fusion.1), channel_id=1, source_target_pairs={{0,1},{1,2},{2,3},{3,4},{4,5},{5,6},{6,7},{8,9},{9,10},{10,11},{11... | collective-permute-start | bytes 294920 | tf_op jit(solution)/shard_map/ppermute | solution.py:18
  45.4 3.7 %collective-permute-done.7 = f32[3,1,4,4,4,128]{5,4,3,2,1,0:T(4,128)S(1)} collective-permute-done((f32[3,1,4,4,4,128]{5,4,3,2,1,0:T(4,128)S(1)}, f32[3,1,4,4,4,128]{5,4,3,2,1,0:T(4,128)S(1)}, u32[]{:S(2)}, u32[]{:S(2)}) %collective-permute-start.7) | collective-permute-done | bytes 98336 | tf_op jit(solution)/shard_map/ppermute | solution.py:19
  49.9 8.2 %fusion.64 = f32[8,4,128]{2,1,0:T(4,128)S(1)} fusion(f32[8,14,4,128]{3,2,1,0:T(4,128)S(1)} %bitcast.440, f32[1,1,8,14,128,128]{5,4,3,2,1,0:T(8,128)} %param.16, f32[1,1,8,4,128]{4,3,2,1,0:T(4,128)S(1)} %copy-done.3, f32[8,4,128]{2,1,0:T(4,128)S(1)} %get-tuple-element.10, f32[8,128]{1,0:T(8,128)S(1)} %bitcast.467), kind=kOutput, calls=%fused_computation.50 | convolution fusion | flops 88092672 | bytes 7622656 | tf_op jit(solution)/shard_map/bkij,bkrj->bri/dot_general | solution.py:35
  59.4 3.3 %collective-permute-start.8 = (f32[1,1,4,2,4,128]{5,4,3,2,1,0:T(4,128)S(1)}, f32[1,1,4,2,4,128]{5,4,3,2,1,0:T(4,128)S(1)}, u32[]{:S(2)}, u32[]{:S(2)}) collective-permute-start(f32[1,1,4,2,4,128]{5,4,3,2,1,0:T(4,128)S(1)} %copy.90), channel_id=1, source_target_pairs={{0,8},{8,16},{16,24},{1,9},{9,17},{17,25},{2,10},{10,18},{18,26},{... | collective-permute-start | bytes 49160 | tf_op jit(solution)/shard_map/ppermute | solution.py:18
  64.7 3.1 %collective-permute-done.9 = f32[1,1,4,2,4,128]{5,4,3,2,1,0:T(4,128)S(1)} collective-permute-done((f32[1,1,4,2,4,128]{5,4,3,2,1,0:T(4,128)S(1)}, f32[1,1,4,2,4,128]{5,4,3,2,1,0:T(4,128)S(1)}, u32[]{:S(2)}, u32[]{:S(2)}) %collective-permute-start.9) | collective-permute-done | bytes 16416 | tf_op jit(solution)/shard_map/ppermute | solution.py:19
  67.8 3.1 %collective-permute-start.10 = (f32[3,1,4,2,4,128]{5,4,3,2,1,0:T(4,128)S(1)}, f32[3,1,4,2,4,128]{5,4,3,2,1,0:T(4,128)S(1)}, u32[]{:S(2)}, u32[]{:S(2)}) collective-permute-start(f32[3,1,4,2,4,128]{5,4,3,2,1,0:T(4,128)S(1)} %constant_dynamic-update-slice_fusion.10), channel_id=1, source_target_pairs={{0,1},{1,2},{2,3},{3,4},{4,5},{5,6},{6,7},{8,9},{9,10},{10,11},{11... | collective-permute-start | bytes 147464 | tf_op jit(solution)/shard_map/ppermute | solution.py:18
  72.3 3.5 %collective-permute-done.11 = f32[3,1,4,2,4,128]{5,4,3,2,1,0:T(4,128)S(1)} collective-permute-done((f32[3,1,4,2,4,128]{5,4,3,2,1,0:T(4,128)S(1)}, f32[3,1,4,2,4,128]{5,4,3,2,1,0:T(4,128)S(1)}, u32[]{:S(2)}, u32[]{:S(2)}) %collective-permute-start.11) | collective-permute-done | bytes 49184 | tf_op jit(solution)/shard_map/ppermute | solution.py:19
  78.7 3.4 %collective-permute-start.12 = (f32[1,1,4,2,4,128]{5,4,3,2,1,0:T(4,128)S(1)}, f32[1,1,4,2,4,128]{5,4,3,2,1,0:T(4,128)S(1)}, u32[]{:S(2)}, u32[]{:S(2)}) collective-permute-start(f32[1,1,4,2,4,128]{5,4,3,2,1,0:T(4,128)S(1)} %copy.95), channel_id=1, source_target_pairs={{0,8},{8,16},{16,24},{1,9},{9,17},{17,25},{2,10},{10,18},{18,26},{... | collective-permute-start | bytes 49160 | tf_op jit(solution)/shard_map/ppermute | solution.py:18
  84.0 3.1 %collective-permute-done.13 = f32[1,1,4,2,4,128]{5,4,3,2,1,0:T(4,128)S(1)} collective-permute-done((f32[1,1,4,2,4,128]{5,4,3,2,1,0:T(4,128)S(1)}, f32[1,1,4,2,4,128]{5,4,3,2,1,0:T(4,128)S(1)}, u32[]{:S(2)}, u32[]{:S(2)}) %collective-permute-start.13) | collective-permute-done | bytes 16416 | tf_op jit(solution)/shard_map/ppermute | solution.py:19
  87.1 4.0 %collective-permute-start.14 = (f32[3,1,4,2,4,128]{5,4,3,2,1,0:T(4,128)S(1)}, f32[3,1,4,2,4,128]{5,4,3,2,1,0:T(4,128)S(1)}, u32[]{:S(2)}, u32[]{:S(2)}) collective-permute-start(f32[3,1,4,2,4,128]{5,4,3,2,1,0:T(4,128)S(1)} %constant_dynamic-update-slice_fusion.18), channel_id=1, source_target_pairs={{0,1},{1,2},{2,3},{3,4},{4,5},{5,6},{6,7},{8,9},{9,10},{10,11},{11... | collective-permute-start | bytes 147464 | tf_op jit(solution)/shard_map/ppermute | solution.py:18
  92.5 3.5 %collective-permute-done.15 = f32[3,1,4,2,4,128]{5,4,3,2,1,0:T(4,128)S(1)} collective-permute-done((f32[3,1,4,2,4,128]{5,4,3,2,1,0:T(4,128)S(1)}, f32[3,1,4,2,4,128]{5,4,3,2,1,0:T(4,128)S(1)}, u32[]{:S(2)}, u32[]{:S(2)}) %collective-permute-start.15) | collective-permute-done | bytes 49184 | tf_op jit(solution)/shard_map/ppermute | solution.py:19
  98.7 39.2 %psum.7 = f32[4,1024]{1,0:T(4,128)S(1)} all-reduce(f32[4,1024]{1,0:T(4,128)S(1)} %bitcast.470), channel_id=1, replica_groups=mesh['row'=4,'col'=8] {'row','col'}, use_global_device_ids=true, to_apply=%region_0.0 | all-reduce | flops 4096 | bytes 32768 | tf_op jit(solution)/shard_map/psum | solution.py:79
  138.1 61.0 %all-gather = f32[32,32,4]{1,2,0:T(4,128)S(1)} all-gather(f32[1,32,4]{1,2,0:T(4,128)S(1)} %convolution_bitcast_fusion.1), channel_id=1, replica_groups=mesh['row'=4,'col'=8] {'row','col'}, dimensions={0}, use_global_device_ids=true | all-gather | bytes 16896 | tf_op jit(solution)/shard_map/all_gather | solution.py:81
  200.3 8.7 %collective-permute-start.16 = (f32[1,1,4,2,4,128]{5,4,3,2,1,0:T(4,128)S(1)}, f32[1,1,4,2,4,128]{5,4,3,2,1,0:T(4,128)S(1)}, u32[]{:S(2)}, u32[]{:S(2)}) collective-permute-start(f32[1,1,4,2,4,128]{5,4,3,2,1,0:T(4,128)S(1)} %copy.103), channel_id=1, source_target_pairs={{0,8},{8,16},{16,24},{1,9},{9,17},{17,25},{2,10},{10,18},{18,26},{... | collective-permute-start | bytes 49160 | tf_op jit(solution)/shard_map/ppermute | solution.py:18
  214.1 3.4 %collective-permute-start.18 = (f32[3,1,4,2,4,128]{5,4,3,2,1,0:T(4,128)S(1)}, f32[3,1,4,2,4,128]{5,4,3,2,1,0:T(4,128)S(1)}, u32[]{:S(2)}, u32[]{:S(2)}) collective-permute-start(f32[3,1,4,2,4,128]{5,4,3,2,1,0:T(4,128)S(1)} %constant_dynamic-update-slice_fusion.26), channel_id=1, source_target_pairs={{0,1},{1,2},{2,3},{3,4},{4,5},{5,6},{6,7},{8,9},{9,10},{10,11},{11... | collective-permute-start | bytes 147464 | tf_op jit(solution)/shard_map/ppermute | solution.py:18
  218.8 3.5 %collective-permute-done.19 = f32[3,1,4,2,4,128]{5,4,3,2,1,0:T(4,128)S(1)} collective-permute-done((f32[3,1,4,2,4,128]{5,4,3,2,1,0:T(4,128)S(1)}, f32[3,1,4,2,4,128]{5,4,3,2,1,0:T(4,128)S(1)}, u32[]{:S(2)}, u32[]{:S(2)}) %collective-permute-start.19) | collective-permute-done | bytes 49184 | tf_op jit(solution)/shard_map/ppermute | solution.py:19
  225.1 3.4 %collective-permute-start.20 = (f32[1,1,4,2,4,128]{5,4,3,2,1,0:T(4,128)S(1)}, f32[1,1,4,2,4,128]{5,4,3,2,1,0:T(4,128)S(1)}, u32[]{:S(2)}, u32[]{:S(2)}) collective-permute-start(f32[1,1,4,2,4,128]{5,4,3,2,1,0:T(4,128)S(1)} %copy.108), channel_id=1, source_target_pairs={{0,8},{8,16},{16,24},{1,9},{9,17},{17,25},{2,10},{10,18},{18,26},{... | collective-permute-start | bytes 49160 | tf_op jit(solution)/shard_map/ppermute | solution.py:18
  237.4 3.5 %collective-permute-done.23 = f32[3,1,4,2,4,128]{5,4,3,2,1,0:T(4,128)S(1)} collective-permute-done((f32[3,1,4,2,4,128]{5,4,3,2,1,0:T(4,128)S(1)}, f32[3,1,4,2,4,128]{5,4,3,2,1,0:T(4,128)S(1)}, u32[]{:S(2)}, u32[]{:S(2)}) %collective-permute-start.23) | collective-permute-done | bytes 49184 | tf_op jit(solution)/shard_map/ppermute | solution.py:19
  244.9 3.4 %collective-permute-start.24 = (f32[1,1,4,4,4,128]{5,4,3,2,1,0:T(4,128)S(1)}, f32[1,1,4,4,4,128]{5,4,3,2,1,0:T(4,128)S(1)}, u32[]{:S(2)}, u32[]{:S(2)}) collective-permute-start(f32[1,1,4,4,4,128]{5,4,3,2,1,0:T(4,128)S(1)} %bitcast.462), channel_id=1, source_target_pairs={{0,8},{8,16},{16,24},{1,9},{9,17},{17,25},{2,10},{10,18},{18,26},{... | collective-permute-start | bytes 98312 | tf_op jit(solution)/shard_map/ppermute | solution.py:18
  250.2 3.3 %collective-permute-done.25 = f32[1,1,4,4,4,128]{5,4,3,2,1,0:T(4,128)S(1)} collective-permute-done((f32[1,1,4,4,4,128]{5,4,3,2,1,0:T(4,128)S(1)}, f32[1,1,4,4,4,128]{5,4,3,2,1,0:T(4,128)S(1)}, u32[]{:S(2)}, u32[]{:S(2)}) %collective-permute-start.25) | collective-permute-done | bytes 32800 | tf_op jit(solution)/shard_map/ppermute | solution.py:19
  257.7 3.7 %collective-permute-done.27 = f32[3,1,4,4,4,128]{5,4,3,2,1,0:T(4,128)S(1)} collective-permute-done((f32[3,1,4,4,4,128]{5,4,3,2,1,0:T(4,128)S(1)}, f32[3,1,4,4,4,128]{5,4,3,2,1,0:T(4,128)S(1)}, u32[]{:S(2)}, u32[]{:S(2)}) %collective-permute-start.27) | collective-permute-done | bytes 98336 | tf_op jit(solution)/shard_map/ppermute | solution.py:19
  262.2 8.2 %constant_dynamic-update-slice_fusion.51 = (f32[24,4,128]{2,1,0:T(4,128)S(1)}, f32[8,4,128]{2,1,0:T(4,128)S(1)}) fusion(f32[8,4,128]{2,1,0:T(4,128)S(1)} %get-tuple-element.18, f32[8,14,4,128]{3,2,1,0:T(4,128)S(1)} %bitcast.437, f32[1,1,8,14,128,128]{5,4,3,2,1,0:T(8,128)} %param.16, f32[8,128]{1,0:T(8,128)S(1)} %bitcast.468, ...), kind=kOutput, calls=%fused_computation.136 | convolution fusion | flops 88104960 | bytes 7639040 | tf_op jit(solution)/shard_map/bkij,bkrj->bri/dot_general | solution.py:35
  271.0 3.3 %collective-permute-start.28 = (f32[1,1,4,4,4,128]{5,4,3,2,1,0:T(4,128)S(1)}, f32[1,1,4,4,4,128]{5,4,3,2,1,0:T(4,128)S(1)}, u32[]{:S(2)}, u32[]{:S(2)}) collective-permute-start(f32[1,1,4,4,4,128]{5,4,3,2,1,0:T(4,128)S(1)} %bitcast.459), channel_id=1, source_target_pairs={{0,8},{8,16},{16,24},{1,9},{9,17},{17,25},{2,10},{10,18},{18,26},{... | collective-permute-start | bytes 98312 | tf_op jit(solution)/shard_map/ppermute | solution.py:18
  276.3 3.3 %collective-permute-done.29 = f32[1,1,4,4,4,128]{5,4,3,2,1,0:T(4,128)S(1)} collective-permute-done((f32[1,1,4,4,4,128]{5,4,3,2,1,0:T(4,128)S(1)}, f32[1,1,4,4,4,128]{5,4,3,2,1,0:T(4,128)S(1)}, u32[]{:S(2)}, u32[]{:S(2)}) %collective-permute-start.29) | collective-permute-done | bytes 32800 | tf_op jit(solution)/shard_map/ppermute | solution.py:19
  283.8 3.7 %collective-permute-done.31 = f32[3,1,4,4,4,128]{5,4,3,2,1,0:T(4,128)S(1)} collective-permute-done((f32[3,1,4,4,4,128]{5,4,3,2,1,0:T(4,128)S(1)}, f32[3,1,4,4,4,128]{5,4,3,2,1,0:T(4,128)S(1)}, u32[]{:S(2)}, u32[]{:S(2)}) %collective-permute-start.31) | collective-permute-done | bytes 98336 | tf_op jit(solution)/shard_map/ppermute | solution.py:19
  288.3 8.8 %fusion.43 = f32[1,1,8,4,128]{4,3,2,1,0:T(4,128)} fusion(f32[8,4,128]{2,1,0:T(4,128)S(1)} %get-tuple-element.20, f32[8,14,4,128]{3,2,1,0:T(4,128)S(1)} %bitcast.439, f32[1,1,8,14,128,128]{5,4,3,2,1,0:T(8,128)} %param.16, f32[1,1,8,4,128]{4,3,2,1,0:T(4,128)S(1)} %copy-done.3, f32[8,128]{1,0:T(8,128)S(1)} %bitcast.469), kind=kOutput, calls=%fused_computation.43 | convolution fusion | flops 88104960 | bytes 7622656 | tf_op jit(solution)/shard_map/bkij,bkrj->bri/dot_general | solution.py:35
  (160 shorter events, 66.7 us)
Async XLA Ops:
  3.1 7.2 %collective-permute-start = (f32[1,1,4,4,4,128]{5,4,3,2,1,0:T(4,128)S(1)}, f32[1,1,4,4,4,128]{5,4,3,2,1,0:T(4,128)S(1)}, u32[]{:S(2)}, u32[]{:S(2)}) collective-permute-start(f32[1,1,4,4,4,128]{5,4,3,2,1,0:T(4,128)S(1)} %bitcast.453), channel_id=1, source_target_pairs={{0,8},{8,16},{16,24},{1,9},{9,17},{17,25},{2,10},{10,18},{18,26},{... | collective-permute-start | bytes 98312 | tf_op jit(solution)/shard_map/ppermute | solution.py:18
  7.6 5.2 %collective-permute-start.1 = (f32[1,1,4,4,4,128]{5,4,3,2,1,0:T(4,128)S(1)}, f32[1,1,4,4,4,128]{5,4,3,2,1,0:T(4,128)S(1)}, u32[]{:S(2)}, u32[]{:S(2)}) collective-permute-start(f32[1,1,4,4,4,128]{5,4,3,2,1,0:T(4,128)S(1)} %bitcast.454), channel_id=1, source_target_pairs={{8,0},{16,8},{24,16},{9,1},{17,9},{25,17},{10,2},{18,10},{26,18},{... | collective-permute-start | bytes 98312 | tf_op jit(solution)/shard_map/ppermute | solution.py:19
  12.9 4.8 %collective-permute-start.2 = (f32[3,1,4,4,4,128]{5,4,3,2,1,0:T(4,128)S(1)}, f32[3,1,4,4,4,128]{5,4,3,2,1,0:T(4,128)S(1)}, u32[]{:S(2)}, u32[]{:S(2)}) collective-permute-start(f32[3,1,4,4,4,128]{5,4,3,2,1,0:T(4,128)S(1)} %pad_maximum_fusion), channel_id=1, source_target_pairs={{0,1},{1,2},{2,3},{3,4},{4,5},{5,6},{6,7},{8,9},{9,10},{10,11},{11... | collective-permute-start | bytes 294920 | tf_op jit(solution)/shard_map/ppermute | solution.py:18
  16.1 5.4 %collective-permute-start.3 = (f32[3,1,4,4,4,128]{5,4,3,2,1,0:T(4,128)S(1)}, f32[3,1,4,4,4,128]{5,4,3,2,1,0:T(4,128)S(1)}, u32[]{:S(2)}, u32[]{:S(2)}) collective-permute-start(f32[3,1,4,4,4,128]{5,4,3,2,1,0:T(4,128)S(1)} %pad_maximum_fusion), channel_id=1, source_target_pairs={{1,0},{2,1},{3,2},{4,3},{5,4},{6,5},{7,6},{9,8},{10,9},{11,10},{12... | collective-permute-start | bytes 294920 | tf_op jit(solution)/shard_map/ppermute | solution.py:19
  31.1 5.4 %collective-permute-start.4 = (f32[1,1,4,4,4,128]{5,4,3,2,1,0:T(4,128)S(1)}, f32[1,1,4,4,4,128]{5,4,3,2,1,0:T(4,128)S(1)}, u32[]{:S(2)}, u32[]{:S(2)}) collective-permute-start(f32[1,1,4,4,4,128]{5,4,3,2,1,0:T(4,128)S(1)} %bitcast.456), channel_id=1, source_target_pairs={{0,8},{8,16},{16,24},{1,9},{9,17},{17,25},{2,10},{10,18},{18,26},{... | collective-permute-start | bytes 98312 | tf_op jit(solution)/shard_map/ppermute | solution.py:18
  34.5 5.2 %collective-permute-start.5 = (f32[1,1,4,4,4,128]{5,4,3,2,1,0:T(4,128)S(1)}, f32[1,1,4,4,4,128]{5,4,3,2,1,0:T(4,128)S(1)}, u32[]{:S(2)}, u32[]{:S(2)}) collective-permute-start(f32[1,1,4,4,4,128]{5,4,3,2,1,0:T(4,128)S(1)} %bitcast.457), channel_id=1, source_target_pairs={{8,0},{16,8},{24,16},{9,1},{17,9},{25,17},{10,2},{18,10},{26,18},{... | collective-permute-start | bytes 98312 | tf_op jit(solution)/shard_map/ppermute | solution.py:19
  39.7 5.7 %collective-permute-start.6 = (f32[3,1,4,4,4,128]{5,4,3,2,1,0:T(4,128)S(1)}, f32[3,1,4,4,4,128]{5,4,3,2,1,0:T(4,128)S(1)}, u32[]{:S(2)}, u32[]{:S(2)}) collective-permute-start(f32[3,1,4,4,4,128]{5,4,3,2,1,0:T(4,128)S(1)} %pad_maximum_fusion.1), channel_id=1, source_target_pairs={{0,1},{1,2},{2,3},{3,4},{4,5},{5,6},{6,7},{8,9},{9,10},{10,11},{11... | collective-permute-start | bytes 294920 | tf_op jit(solution)/shard_map/ppermute | solution.py:18
  43.8 5.4 %collective-permute-start.7 = (f32[3,1,4,4,4,128]{5,4,3,2,1,0:T(4,128)S(1)}, f32[3,1,4,4,4,128]{5,4,3,2,1,0:T(4,128)S(1)}, u32[]{:S(2)}, u32[]{:S(2)}) collective-permute-start(f32[3,1,4,4,4,128]{5,4,3,2,1,0:T(4,128)S(1)} %pad_maximum_fusion.1), channel_id=1, source_target_pairs={{1,0},{2,1},{3,2},{4,3},{5,4},{6,5},{7,6},{9,8},{10,9},{11,10},{12... | collective-permute-start | bytes 294920 | tf_op jit(solution)/shard_map/ppermute | solution.py:19
  59.4 5.3 %collective-permute-start.8 = (f32[1,1,4,2,4,128]{5,4,3,2,1,0:T(4,128)S(1)}, f32[1,1,4,2,4,128]{5,4,3,2,1,0:T(4,128)S(1)}, u32[]{:S(2)}, u32[]{:S(2)}) collective-permute-start(f32[1,1,4,2,4,128]{5,4,3,2,1,0:T(4,128)S(1)} %copy.90), channel_id=1, source_target_pairs={{0,8},{8,16},{16,24},{1,9},{9,17},{17,25},{2,10},{10,18},{18,26},{... | collective-permute-start | bytes 49160 | tf_op jit(solution)/shard_map/ppermute | solution.py:18
  62.8 5.1 %collective-permute-start.9 = (f32[1,1,4,2,4,128]{5,4,3,2,1,0:T(4,128)S(1)}, f32[1,1,4,2,4,128]{5,4,3,2,1,0:T(4,128)S(1)}, u32[]{:S(2)}, u32[]{:S(2)}) collective-permute-start(f32[1,1,4,2,4,128]{5,4,3,2,1,0:T(4,128)S(1)} %copy.90), channel_id=1, source_target_pairs={{8,0},{16,8},{24,16},{9,1},{17,9},{25,17},{10,2},{18,10},{26,18},{... | collective-permute-start | bytes 49160 | tf_op jit(solution)/shard_map/ppermute | solution.py:19
  67.8 4.5 %collective-permute-start.10 = (f32[3,1,4,2,4,128]{5,4,3,2,1,0:T(4,128)S(1)}, f32[3,1,4,2,4,128]{5,4,3,2,1,0:T(4,128)S(1)}, u32[]{:S(2)}, u32[]{:S(2)}) collective-permute-start(f32[3,1,4,2,4,128]{5,4,3,2,1,0:T(4,128)S(1)} %constant_dynamic-update-slice_fusion.10), channel_id=1, source_target_pairs={{0,1},{1,2},{2,3},{3,4},{4,5},{5,6},{6,7},{8,9},{9,10},{10,11},{11... | collective-permute-start | bytes 147464 | tf_op jit(solution)/shard_map/ppermute | solution.py:18
  71.0 4.8 %collective-permute-start.11 = (f32[3,1,4,2,4,128]{5,4,3,2,1,0:T(4,128)S(1)}, f32[3,1,4,2,4,128]{5,4,3,2,1,0:T(4,128)S(1)}, u32[]{:S(2)}, u32[]{:S(2)}) collective-permute-start(f32[3,1,4,2,4,128]{5,4,3,2,1,0:T(4,128)S(1)} %constant_dynamic-update-slice_fusion.10), channel_id=1, source_target_pairs={{1,0},{2,1},{3,2},{4,3},{5,4},{6,5},{7,6},{9,8},{10,9},{11,10},{12... | collective-permute-start | bytes 147464 | tf_op jit(solution)/shard_map/ppermute | solution.py:19
  78.7 5.3 %collective-permute-start.12 = (f32[1,1,4,2,4,128]{5,4,3,2,1,0:T(4,128)S(1)}, f32[1,1,4,2,4,128]{5,4,3,2,1,0:T(4,128)S(1)}, u32[]{:S(2)}, u32[]{:S(2)}) collective-permute-start(f32[1,1,4,2,4,128]{5,4,3,2,1,0:T(4,128)S(1)} %copy.95), channel_id=1, source_target_pairs={{0,8},{8,16},{16,24},{1,9},{9,17},{17,25},{2,10},{10,18},{18,26},{... | collective-permute-start | bytes 49160 | tf_op jit(solution)/shard_map/ppermute | solution.py:18
  82.0 5.1 %collective-permute-start.13 = (f32[1,1,4,2,4,128]{5,4,3,2,1,0:T(4,128)S(1)}, f32[1,1,4,2,4,128]{5,4,3,2,1,0:T(4,128)S(1)}, u32[]{:S(2)}, u32[]{:S(2)}) collective-permute-start(f32[1,1,4,2,4,128]{5,4,3,2,1,0:T(4,128)S(1)} %copy.95), channel_id=1, source_target_pairs={{8,0},{16,8},{24,16},{9,1},{17,9},{25,17},{10,2},{18,10},{26,18},{... | collective-permute-start | bytes 49160 | tf_op jit(solution)/shard_map/ppermute | solution.py:19
  87.1 5.4 %collective-permute-start.14 = (f32[3,1,4,2,4,128]{5,4,3,2,1,0:T(4,128)S(1)}, f32[3,1,4,2,4,128]{5,4,3,2,1,0:T(4,128)S(1)}, u32[]{:S(2)}, u32[]{:S(2)}) collective-permute-start(f32[3,1,4,2,4,128]{5,4,3,2,1,0:T(4,128)S(1)} %constant_dynamic-update-slice_fusion.18), channel_id=1, source_target_pairs={{0,1},{1,2},{2,3},{3,4},{4,5},{5,6},{6,7},{8,9},{9,10},{10,11},{11... | collective-permute-start | bytes 147464 | tf_op jit(solution)/shard_map/ppermute | solution.py:18
  91.1 4.8 %collective-permute-start.15 = (f32[3,1,4,2,4,128]{5,4,3,2,1,0:T(4,128)S(1)}, f32[3,1,4,2,4,128]{5,4,3,2,1,0:T(4,128)S(1)}, u32[]{:S(2)}, u32[]{:S(2)}) collective-permute-start(f32[3,1,4,2,4,128]{5,4,3,2,1,0:T(4,128)S(1)} %constant_dynamic-update-slice_fusion.18), channel_id=1, source_target_pairs={{1,0},{2,1},{3,2},{4,3},{5,4},{6,5},{7,6},{9,8},{10,9},{11,10},{12... | collective-permute-start | bytes 147464 | tf_op jit(solution)/shard_map/ppermute | solution.py:19
  200.3 10.6 %collective-permute-start.16 = (f32[1,1,4,2,4,128]{5,4,3,2,1,0:T(4,128)S(1)}, f32[1,1,4,2,4,128]{5,4,3,2,1,0:T(4,128)S(1)}, u32[]{:S(2)}, u32[]{:S(2)}) collective-permute-start(f32[1,1,4,2,4,128]{5,4,3,2,1,0:T(4,128)S(1)} %copy.103), channel_id=1, source_target_pairs={{0,8},{8,16},{16,24},{1,9},{9,17},{17,25},{2,10},{10,18},{18,26},{... | collective-permute-start | bytes 49160 | tf_op jit(solution)/shard_map/ppermute | solution.py:18
  209.0 5.1 %collective-permute-start.17 = (f32[1,1,4,2,4,128]{5,4,3,2,1,0:T(4,128)S(1)}, f32[1,1,4,2,4,128]{5,4,3,2,1,0:T(4,128)S(1)}, u32[]{:S(2)}, u32[]{:S(2)}) collective-permute-start(f32[1,1,4,2,4,128]{5,4,3,2,1,0:T(4,128)S(1)} %copy.103), channel_id=1, source_target_pairs={{8,0},{16,8},{24,16},{9,1},{17,9},{25,17},{10,2},{18,10},{26,18},{... | collective-permute-start | bytes 49160 | tf_op jit(solution)/shard_map/ppermute | solution.py:19
  214.1 4.7 %collective-permute-start.18 = (f32[3,1,4,2,4,128]{5,4,3,2,1,0:T(4,128)S(1)}, f32[3,1,4,2,4,128]{5,4,3,2,1,0:T(4,128)S(1)}, u32[]{:S(2)}, u32[]{:S(2)}) collective-permute-start(f32[3,1,4,2,4,128]{5,4,3,2,1,0:T(4,128)S(1)} %constant_dynamic-update-slice_fusion.26), channel_id=1, source_target_pairs={{0,1},{1,2},{2,3},{3,4},{4,5},{5,6},{6,7},{8,9},{9,10},{10,11},{11... | collective-permute-start | bytes 147464 | tf_op jit(solution)/shard_map/ppermute | solution.py:18
  217.5 4.8 %collective-permute-start.19 = (f32[3,1,4,2,4,128]{5,4,3,2,1,0:T(4,128)S(1)}, f32[3,1,4,2,4,128]{5,4,3,2,1,0:T(4,128)S(1)}, u32[]{:S(2)}, u32[]{:S(2)}) collective-permute-start(f32[3,1,4,2,4,128]{5,4,3,2,1,0:T(4,128)S(1)} %constant_dynamic-update-slice_fusion.26), channel_id=1, source_target_pairs={{1,0},{2,1},{3,2},{4,3},{5,4},{6,5},{7,6},{9,8},{10,9},{11,10},{12... | collective-permute-start | bytes 147464 | tf_op jit(solution)/shard_map/ppermute | solution.py:19
  225.1 5.3 %collective-permute-start.20 = (f32[1,1,4,2,4,128]{5,4,3,2,1,0:T(4,128)S(1)}, f32[1,1,4,2,4,128]{5,4,3,2,1,0:T(4,128)S(1)}, u32[]{:S(2)}, u32[]{:S(2)}) collective-permute-start(f32[1,1,4,2,4,128]{5,4,3,2,1,0:T(4,128)S(1)} %copy.108), channel_id=1, source_target_pairs={{0,8},{8,16},{16,24},{1,9},{9,17},{17,25},{2,10},{10,18},{18,26},{... | collective-permute-start | bytes 49160 | tf_op jit(solution)/shard_map/ppermute | solution.py:18
  228.5 5.1 %collective-permute-start.21 = (f32[1,1,4,2,4,128]{5,4,3,2,1,0:T(4,128)S(1)}, f32[1,1,4,2,4,128]{5,4,3,2,1,0:T(4,128)S(1)}, u32[]{:S(2)}, u32[]{:S(2)}) collective-permute-start(f32[1,1,4,2,4,128]{5,4,3,2,1,0:T(4,128)S(1)} %copy.108), channel_id=1, source_target_pairs={{8,0},{16,8},{24,16},{9,1},{17,9},{25,17},{10,2},{18,10},{26,18},{... | collective-permute-start | bytes 49160 | tf_op jit(solution)/shard_map/ppermute | solution.py:19
  233.6 3.9 %collective-permute-start.22 = (f32[3,1,4,2,4,128]{5,4,3,2,1,0:T(4,128)S(1)}, f32[3,1,4,2,4,128]{5,4,3,2,1,0:T(4,128)S(1)}, u32[]{:S(2)}, u32[]{:S(2)}) collective-permute-start(f32[3,1,4,2,4,128]{5,4,3,2,1,0:T(4,128)S(1)} %constant_dynamic-update-slice_fusion.34), channel_id=1, source_target_pairs={{0,1},{1,2},{2,3},{3,4},{4,5},{5,6},{6,7},{8,9},{9,10},{10,11},{11... | collective-permute-start | bytes 147464 | tf_op jit(solution)/shard_map/ppermute | solution.py:18
  236.1 4.8 %collective-permute-start.23 = (f32[3,1,4,2,4,128]{5,4,3,2,1,0:T(4,128)S(1)}, f32[3,1,4,2,4,128]{5,4,3,2,1,0:T(4,128)S(1)}, u32[]{:S(2)}, u32[]{:S(2)}) collective-permute-start(f32[3,1,4,2,4,128]{5,4,3,2,1,0:T(4,128)S(1)} %constant_dynamic-update-slice_fusion.34), channel_id=1, source_target_pairs={{1,0},{2,1},{3,2},{4,3},{5,4},{6,5},{7,6},{9,8},{10,9},{11,10},{12... | collective-permute-start | bytes 147464 | tf_op jit(solution)/shard_map/ppermute | solution.py:19
  244.9 5.3 %collective-permute-start.24 = (f32[1,1,4,4,4,128]{5,4,3,2,1,0:T(4,128)S(1)}, f32[1,1,4,4,4,128]{5,4,3,2,1,0:T(4,128)S(1)}, u32[]{:S(2)}, u32[]{:S(2)}) collective-permute-start(f32[1,1,4,4,4,128]{5,4,3,2,1,0:T(4,128)S(1)} %bitcast.462), channel_id=1, source_target_pairs={{0,8},{8,16},{16,24},{1,9},{9,17},{17,25},{2,10},{10,18},{18,26},{... | collective-permute-start | bytes 98312 | tf_op jit(solution)/shard_map/ppermute | solution.py:18
  248.3 5.2 %collective-permute-start.25 = (f32[1,1,4,4,4,128]{5,4,3,2,1,0:T(4,128)S(1)}, f32[1,1,4,4,4,128]{5,4,3,2,1,0:T(4,128)S(1)}, u32[]{:S(2)}, u32[]{:S(2)}) collective-permute-start(f32[1,1,4,4,4,128]{5,4,3,2,1,0:T(4,128)S(1)} %bitcast.463), channel_id=1, source_target_pairs={{8,0},{16,8},{24,16},{9,1},{17,9},{25,17},{10,2},{18,10},{26,18},{... | collective-permute-start | bytes 98312 | tf_op jit(solution)/shard_map/ppermute | solution.py:19
  253.5 4.2 %collective-permute-start.26 = (f32[3,1,4,4,4,128]{5,4,3,2,1,0:T(4,128)S(1)}, f32[3,1,4,4,4,128]{5,4,3,2,1,0:T(4,128)S(1)}, u32[]{:S(2)}, u32[]{:S(2)}) collective-permute-start(f32[3,1,4,4,4,128]{5,4,3,2,1,0:T(4,128)S(1)} %pad_maximum_fusion.2), channel_id=1, source_target_pairs={{0,1},{1,2},{2,3},{3,4},{4,5},{5,6},{6,7},{8,9},{9,10},{10,11},{11... | collective-permute-start | bytes 294920 | tf_op jit(solution)/shard_map/ppermute | solution.py:18
  256.1 5.4 %collective-permute-start.27 = (f32[3,1,4,4,4,128]{5,4,3,2,1,0:T(4,128)S(1)}, f32[3,1,4,4,4,128]{5,4,3,2,1,0:T(4,128)S(1)}, u32[]{:S(2)}, u32[]{:S(2)}) collective-permute-start(f32[3,1,4,4,4,128]{5,4,3,2,1,0:T(4,128)S(1)} %pad_maximum_fusion.2), channel_id=1, source_target_pairs={{1,0},{2,1},{3,2},{4,3},{5,4},{6,5},{7,6},{9,8},{10,9},{11,10},{12... | collective-permute-start | bytes 294920 | tf_op jit(solution)/shard_map/ppermute | solution.py:19
  271.0 5.3 %collective-permute-start.28 = (f32[1,1,4,4,4,128]{5,4,3,2,1,0:T(4,128)S(1)}, f32[1,1,4,4,4,128]{5,4,3,2,1,0:T(4,128)S(1)}, u32[]{:S(2)}, u32[]{:S(2)}) collective-permute-start(f32[1,1,4,4,4,128]{5,4,3,2,1,0:T(4,128)S(1)} %bitcast.459), channel_id=1, source_target_pairs={{0,8},{8,16},{16,24},{1,9},{9,17},{17,25},{2,10},{10,18},{18,26},{... | collective-permute-start | bytes 98312 | tf_op jit(solution)/shard_map/ppermute | solution.py:18
  274.4 5.2 %collective-permute-start.29 = (f32[1,1,4,4,4,128]{5,4,3,2,1,0:T(4,128)S(1)}, f32[1,1,4,4,4,128]{5,4,3,2,1,0:T(4,128)S(1)}, u32[]{:S(2)}, u32[]{:S(2)}) collective-permute-start(f32[1,1,4,4,4,128]{5,4,3,2,1,0:T(4,128)S(1)} %bitcast.460), channel_id=1, source_target_pairs={{8,0},{16,8},{24,16},{9,1},{17,9},{25,17},{10,2},{18,10},{26,18},{... | collective-permute-start | bytes 98312 | tf_op jit(solution)/shard_map/ppermute | solution.py:19
  279.6 4.2 %collective-permute-start.30 = (f32[3,1,4,4,4,128]{5,4,3,2,1,0:T(4,128)S(1)}, f32[3,1,4,4,4,128]{5,4,3,2,1,0:T(4,128)S(1)}, u32[]{:S(2)}, u32[]{:S(2)}) collective-permute-start(f32[3,1,4,4,4,128]{5,4,3,2,1,0:T(4,128)S(1)} %pad_maximum_fusion.3), channel_id=1, source_target_pairs={{0,1},{1,2},{2,3},{3,4},{4,5},{5,6},{6,7},{8,9},{9,10},{10,11},{11... | collective-permute-start | bytes 294920 | tf_op jit(solution)/shard_map/ppermute | solution.py:18
  282.2 5.4 %collective-permute-start.31 = (f32[3,1,4,4,4,128]{5,4,3,2,1,0:T(4,128)S(1)}, f32[3,1,4,4,4,128]{5,4,3,2,1,0:T(4,128)S(1)}, u32[]{:S(2)}, u32[]{:S(2)}) collective-permute-start(f32[3,1,4,4,4,128]{5,4,3,2,1,0:T(4,128)S(1)} %pad_maximum_fusion.3), channel_id=1, source_target_pairs={{1,0},{2,1},{3,2},{4,3},{5,4},{6,5},{7,6},{9,8},{10,9},{11,10},{12... | collective-permute-start | bytes 294920 | tf_op jit(solution)/shard_map/ppermute | solution.py:19
  (10 other events, 564.7 us)
where the time goes:
time: 298 us; the launch traced here: 297 us
  blocking collectives  100 us (34%)
  starting transfers between devices  84.3 us (28%)
  waiting for transfers between devices  54.8 us (18%)
  matrix products  43 us (14%)
  local copies, waits for them, and re-layouts  11 us (4%)
  other arithmetic  3.06 us (1%)
    all_gather x1, blocking collectives, on_device(): coarse_x = lax.all_gather(own_rows, ('row', 'col'), axis=1, tiled=True)  61 us
    ppermute x16, starting transfers between devices, padded_2(): before = lax.ppermute(last, axis, up)  58.6 us
    ppermute x16, waiting for transfers between devices, padded_2(): after = lax.ppermute(leading, axis, down)  53.6 us
    dot_general x8, matrix products, apply_op(): coupled = jnp.einsum('bkij,bkrj->bri', blocks, nearby, precision=HIGH)  40 us
    psum x1, blocking collectives, on_device(): coarse_rhs = lax.psum(term, ('row', 'col'))  39.2 us
    ppermute x16, starting transfers between devices, padded_2(): after = lax.ppermute(leading, axis, down)  25.7 us
  transfers between devices with their start and end apart: 32, of which 20 were waited for; matrix products, arithmetic and copies ran while one was open for 0% of the time, Pallas kernels for 0%

commit v1 on v0

--- a/solution.py
+++ b/solution.py
@@ -76,7 +76,7 @@
     onehot1 = (agg1[0, 0][:, None] == jnp.arange(coarse_count)).astype(jnp.float32)
     contrib = jnp.einsum("bij,bri->brj", level_pro, level_res, precision=HIGH)
     term = jnp.einsum("bc,brj->rcj", onehot1, contrib, precision=HIGH).reshape(loads, coarse_total)
-    coarse_rhs = lax.psum(term, ("row", "col"))
+    coarse_rhs = jnp.sum(lax.all_gather(term, ("row", "col")), axis=0)
     own_rows = jnp.einsum("ij,rj->ri", cinv, coarse_rhs, precision=HIGH)
     coarse_x = lax.all_gather(own_rows, ("row", "col"), axis=1, tiled=True)
     coarse_blocks = coarse_x.reshape(loads, coarse_count, block_size)

time: 298 us -> 327 us (1.097); the launches traced: 297 us -> 321 us
  blocking collectives: 100 us -> 127 us
  waiting for transfers between devices: 54.8 us -> 31 us
  starting transfers between devices: 84.3 us -> 105 us
    all_gather x0 -> x1, blocking collectives: none -> 66.2 us  [on_device(): coarse_rhs = jnp.sum(lax.all_gather(term, ('row', 'col')), axis=0)]
    ppermute x16, waiting for transfers between devices: 53.6 us -> 12.4 us  [padded_2(): after = lax.ppermute(leading, axis, down)]
    psum x1 -> x0, blocking collectives: 39.2 us -> none  [on_device(): coarse_rhs = lax.psum(term, ('row', 'col'))]
    ppermute x16, starting transfers between devices: 58.6 us -> 78.9 us  [padded_2(): before = lax.ppermute(last, axis, up)]
    ppermute x16, waiting for transfers between devices: 1.2 us -> 18.6 us  [padded_2(): before = lax.ppermute(last, axis, up)]
  transfers between devices with their start and end apart: 32 -> 32, of which waited for: 20 -> 16; matrix products, arithmetic and copies ran while one was open for 0% -> 0% of each run, Pallas kernels for 0% -> 0%
where the time goes in v1:
time: 327 us; the launch traced here: 321 us
  blocking collectives  127 us (39%)
  starting transfers between devices  105 us (32%)
  matrix products  43 us (13%)
  waiting for transfers between devices  31 us (9%)
  local copies, waits for them, and re-layouts  11 us (3%)
    ppermute x16, starting transfers between devices, padded_2(): before = lax.ppermute(last, axis, up)  78.9 us
    all_gather x1, blocking collectives, on_device(): coarse_rhs = jnp.sum(lax.all_gather(term, ('row', 'col')), axis=0)  66.2 us
    all_gather x1, blocking collectives, on_device(): coarse_x = lax.all_gather(own_rows, ('row', 'col'), axis=1, tiled=True)  60.8 us
    dot_general x8, matrix products, apply_op(): coupled = jnp.einsum('bkij,bkrj->bri', blocks, nearby, precision=HIGH)  40 us
    ppermute x16, starting transfers between devices, padded_2(): after = lax.ppermute(leading, axis, down)  26.2 us
    ppermute x16, waiting for transfers between devices, padded_2(): before = lax.ppermute(last, axis, up)  18.6 us
    ppermute x16, waiting for transfers between devices, padded_2(): after = lax.ppermute(leading, axis, down)  12.4 us
  transfers between devices with their start and end apart: 32, of which 16 were waited for; matrix products, arithmetic and copies ran while one was open for 0% of the time, Pallas kernels for 0%

profile of v1, /device:TPU:1, one launch (start us, length us, event | category | flops | bytes accessed | tf_op | source)
XLA Modules:
  0.0 321.1 jit_solution(14593826248141654772)
XLA Ops:
  5.1 4.5 %collective-permute-start = (f32[1,1,4,4,4,128]{5,4,3,2,1,0:T(4,128)S(1)}, f32[1,1,4,4,4,128]{5,4,3,2,1,0:T(4,128)S(1)}, u32[]{:S(2)}, u32[]{:S(2)}) collective-permute-start(f32[1,1,4,4,4,128]{5,4,3,2,1,0:T(4,128)S(1)} %bitcast.450), channel_id=1, source_target_pairs={{0,8},{8,16},{16,24},{1,9},{9,17},{17,25},{2,10},{10,18},{18,26},{... | collective-permute-start | bytes 98312 | tf_op jit(solution)/shard_map/ppermute | solution.py:18
  11.9 4.0 %collective-permute-start.2 = (f32[3,1,4,4,4,128]{5,4,3,2,1,0:T(4,128)S(1)}, f32[3,1,4,4,4,128]{5,4,3,2,1,0:T(4,128)S(1)}, u32[]{:S(2)}, u32[]{:S(2)}) collective-permute-start(f32[3,1,4,4,4,128]{5,4,3,2,1,0:T(4,128)S(1)} %pad_maximum_fusion), channel_id=1, source_target_pairs={{0,1},{1,2},{2,3},{3,4},{4,5},{5,6},{6,7},{8,9},{9,10},{10,11},{11... | collective-permute-start | bytes 294920 | tf_op jit(solution)/shard_map/ppermute | solution.py:18
  15.9 3.2 collective-permute-done.2
  19.9 8.3 %constant_dynamic-update-slice_fusion.9 = (f32[24,4,128]{2,1,0:T(4,128)S(1)}, f32[8,4,128]{2,1,0:T(4,128)S(1)}) fusion(f32[8,14,4,128]{3,2,1,0:T(4,128)S(1)} %bitcast.434, f32[1,1,8,14,128,128]{5,4,3,2,1,0:T(8,128)} %param.16, f32[8,128]{1,0:T(8,128)} %bitcast.462, f32[1,1,8,4,128]{4,3,2,1,0:T(4,128)} %param.14), kind=kOutput, calls=%fused_computation.94 | convolution fusion | flops 88113152 | bytes 7622656 | tf_op jit(solution)/shard_map/bkij,bkrj->bri/dot_general | solution.py:35
  28.8 2.2 collective-permute-start.5
  31.0 3.5 %collective-permute-start.4 = (f32[1,1,4,4,4,128]{5,4,3,2,1,0:T(4,128)S(1)}, f32[1,1,4,4,4,128]{5,4,3,2,1,0:T(4,128)S(1)}, u32[]{:S(2)}, u32[]{:S(2)}) collective-permute-start(f32[1,1,4,4,4,128]{5,4,3,2,1,0:T(4,128)S(1)} %bitcast.453), channel_id=1, source_target_pairs={{0,8},{8,16},{16,24},{1,9},{9,17},{17,25},{2,10},{10,18},{18,26},{... | collective-permute-start | bytes 98312 | tf_op jit(solution)/shard_map/ppermute | solution.py:18
  37.0 4.7 %collective-permute-start.6 = (f32[3,1,4,4,4,128]{5,4,3,2,1,0:T(4,128)S(1)}, f32[3,1,4,4,4,128]{5,4,3,2,1,0:T(4,128)S(1)}, u32[]{:S(2)}, u32[]{:S(2)}) collective-permute-start(f32[3,1,4,4,4,128]{5,4,3,2,1,0:T(4,128)S(1)} %pad_maximum_fusion.1), channel_id=1, source_target_pairs={{0,1},{1,2},{2,3},{3,4},{4,5},{5,6},{6,7},{8,9},{9,10},{10,11},{11... | collective-permute-start | bytes 294920 | tf_op jit(solution)/shard_map/ppermute | solution.py:18
  41.7 2.9 collective-permute-done.6
  45.4 8.2 %fusion.64 = f32[8,4,128]{2,1,0:T(4,128)S(1)} fusion(f32[8,14,4,128]{3,2,1,0:T(4,128)S(1)} %bitcast.436, f32[1,1,8,14,128,128]{5,4,3,2,1,0:T(8,128)} %param.16, f32[1,1,8,4,128]{4,3,2,1,0:T(4,128)S(1)} %copy-done.3, f32[8,4,128]{2,1,0:T(4,128)S(1)} %get-tuple-element.10, f32[8,128]{1,0:T(8,128)S(1)} %bitcast.463), kind=kOutput, calls=%fused_computation.50 | convolution fusion | flops 88092672 | bytes 7622656 | tf_op jit(solution)/shard_map/bkij,bkrj->bri/dot_general | solution.py:35
  54.9 4.1 %collective-permute-start.8 = (f32[1,1,4,2,4,128]{5,4,3,2,1,0:T(4,128)S(1)}, f32[1,1,4,2,4,128]{5,4,3,2,1,0:T(4,128)S(1)}, u32[]{:S(2)}, u32[]{:S(2)}) collective-permute-start(f32[1,1,4,2,4,128]{5,4,3,2,1,0:T(4,128)S(1)} %copy.90), channel_id=1, source_target_pairs={{0,8},{8,16},{16,24},{1,9},{9,17},{17,25},{2,10},{10,18},{18,26},{... | collective-permute-start | bytes 49160 | tf_op jit(solution)/shard_map/ppermute | solution.py:18
  61.0 3.1 collective-permute-done.9
  65.3 5.2 %collective-permute-start.10 = (f32[3,1,4,2,4,128]{5,4,3,2,1,0:T(4,128)S(1)}, f32[3,1,4,2,4,128]{5,4,3,2,1,0:T(4,128)S(1)}, u32[]{:S(2)}, u32[]{:S(2)}) collective-permute-start(f32[3,1,4,2,4,128]{5,4,3,2,1,0:T(4,128)S(1)} %constant_dynamic-update-slice_fusion.10), channel_id=1, source_target_pairs={{0,1},{1,2},{2,3},{3,4},{4,5},{5,6},{6,7},{8,9},{9,10},{10,11},{11... | collective-permute-start | bytes 147464 | tf_op jit(solution)/shard_map/ppermute | solution.py:18
  74.6 2.8 collective-permute-start.12
  79.4 3.1 collective-permute-done.13
  83.7 5.6 %collective-permute-start.14 = (f32[3,1,4,2,4,128]{5,4,3,2,1,0:T(4,128)S(1)}, f32[3,1,4,2,4,128]{5,4,3,2,1,0:T(4,128)S(1)}, u32[]{:S(2)}, u32[]{:S(2)}) collective-permute-start(f32[3,1,4,2,4,128]{5,4,3,2,1,0:T(4,128)S(1)} %constant_dynamic-update-slice_fusion.18), channel_id=1, source_target_pairs={{0,1},{1,2},{2,3},{3,4},{4,5},{5,6},{6,7},{8,9},{9,10},{10,11},{11... | collective-permute-start | bytes 147464 | tf_op jit(solution)/shard_map/ppermute | solution.py:18
  93.2 66.2 %all_gather.6 = f32[32,4,1024]{2,1,0:T(4,128)S(1)} all-gather(f32[1,4,1024]{2,1,0:T(4,128)S(1)} %all_gather_reshape.3), channel_id=1, replica_groups=mesh['row'=4,'col'=8] {'row','col'}, dimensions={0}, use_global_device_ids=true | all-gather | bytes 540672 | tf_op jit(solution)/shard_map/all_gather | solution.py:79
  159.7 60.8 %all-gather = f32[32,32,4]{1,2,0:T(4,128)S(1)} all-gather(f32[1,32,4]{1,2,0:T(4,128)S(1)} %convolution_bitcast_fusion.1), channel_id=1, replica_groups=mesh['row'=4,'col'=8] {'row','col'}, dimensions={0}, use_global_device_ids=true | all-gather | bytes 16896 | tf_op jit(solution)/shard_map/all_gather | solution.py:81
  221.8 14.0 %collective-permute-start.16 = (f32[1,1,4,2,4,128]{5,4,3,2,1,0:T(4,128)S(1)}, f32[1,1,4,2,4,128]{5,4,3,2,1,0:T(4,128)S(1)}, u32[]{:S(2)}, u32[]{:S(2)}) collective-permute-start(f32[1,1,4,2,4,128]{5,4,3,2,1,0:T(4,128)S(1)} %copy.103), channel_id=1, source_target_pairs={{0,8},{8,16},{16,24},{1,9},{9,17},{17,25},{2,10},{10,18},{18,26},{... | collective-permute-start | bytes 49160 | tf_op jit(solution)/shard_map/ppermute | solution.py:18
  237.7 3.1 collective-permute-done.17
  242.1 4.7 %collective-permute-start.18 = (f32[3,1,4,2,4,128]{5,4,3,2,1,0:T(4,128)S(1)}, f32[3,1,4,2,4,128]{5,4,3,2,1,0:T(4,128)S(1)}, u32[]{:S(2)}, u32[]{:S(2)}) collective-permute-start(f32[3,1,4,2,4,128]{5,4,3,2,1,0:T(4,128)S(1)} %constant_dynamic-update-slice_fusion.26), channel_id=1, source_target_pairs={{0,1},{1,2},{2,3},{3,4},{4,5},{5,6},{6,7},{8,9},{9,10},{10,11},{11... | collective-permute-start | bytes 147464 | tf_op jit(solution)/shard_map/ppermute | solution.py:18
  250.6 2.8 collective-permute-start.20
  255.4 3.1 collective-permute-done.21
  259.8 5.2 %collective-permute-start.22 = (f32[3,1,4,2,4,128]{5,4,3,2,1,0:T(4,128)S(1)}, f32[3,1,4,2,4,128]{5,4,3,2,1,0:T(4,128)S(1)}, u32[]{:S(2)}, u32[]{:S(2)}) collective-permute-start(f32[3,1,4,2,4,128]{5,4,3,2,1,0:T(4,128)S(1)} %constant_dynamic-update-slice_fusion.34), channel_id=1, source_target_pairs={{0,1},{1,2},{2,3},{3,4},{4,5},{5,6},{6,7},{8,9},{9,10},{10,11},{11... | collective-permute-start | bytes 147464 | tf_op jit(solution)/shard_map/ppermute | solution.py:18
  272.0 3.6 %collective-permute-start.24 = (f32[1,1,4,4,4,128]{5,4,3,2,1,0:T(4,128)S(1)}, f32[1,1,4,4,4,128]{5,4,3,2,1,0:T(4,128)S(1)}, u32[]{:S(2)}, u32[]{:S(2)}) collective-permute-start(f32[1,1,4,4,4,128]{5,4,3,2,1,0:T(4,128)S(1)} %bitcast.459), channel_id=1, source_target_pairs={{0,8},{8,16},{16,24},{1,9},{9,17},{17,25},{2,10},{10,18},{18,26},{... | collective-permute-start | bytes 98312 | tf_op jit(solution)/shard_map/ppermute | solution.py:18
  278.0 5.5 %collective-permute-start.26 = (f32[3,1,4,4,4,128]{5,4,3,2,1,0:T(4,128)S(1)}, f32[3,1,4,4,4,128]{5,4,3,2,1,0:T(4,128)S(1)}, u32[]{:S(2)}, u32[]{:S(2)}) collective-permute-start(f32[3,1,4,4,4,128]{5,4,3,2,1,0:T(4,128)S(1)} %pad_maximum_fusion.2), channel_id=1, source_target_pairs={{0,1},{1,2},{2,3},{3,4},{4,5},{5,6},{6,7},{8,9},{9,10},{10,11},{11... | collective-permute-start | bytes 294920 | tf_op jit(solution)/shard_map/ppermute | solution.py:18
  283.5 2.8 collective-permute-done.26
  287.1 8.2 %constant_dynamic-update-slice_fusion.51 = (f32[24,4,128]{2,1,0:T(4,128)S(1)}, f32[8,4,128]{2,1,0:T(4,128)S(1)}) fusion(f32[8,4,128]{2,1,0:T(4,128)S(1)} %get-tuple-element.18, f32[8,14,4,128]{3,2,1,0:T(4,128)S(1)} %bitcast.433, f32[1,1,8,14,128,128]{5,4,3,2,1,0:T(8,128)} %param.16, f32[8,128]{1,0:T(8,128)S(1)} %bitcast.464, ...), kind=kOutput, calls=%fused_computation.136 | convolution fusion | flops 88104960 | bytes 7639040 | tf_op jit(solution)/shard_map/bkij,bkrj->bri/dot_general | solution.py:35
  295.9 2.1 collective-permute-start.29
  298.0 3.7 %collective-permute-start.28 = (f32[1,1,4,4,4,128]{5,4,3,2,1,0:T(4,128)S(1)}, f32[1,1,4,4,4,128]{5,4,3,2,1,0:T(4,128)S(1)}, u32[]{:S(2)}, u32[]{:S(2)}) collective-permute-start(f32[1,1,4,4,4,128]{5,4,3,2,1,0:T(4,128)S(1)} %bitcast.456), channel_id=1, source_target_pairs={{0,8},{8,16},{16,24},{1,9},{9,17},{17,25},{2,10},{10,18},{18,26},{... | collective-permute-start | bytes 98312 | tf_op jit(solution)/shard_map/ppermute | solution.py:18
  304.0 5.2 %collective-permute-start.30 = (f32[3,1,4,4,4,128]{5,4,3,2,1,0:T(4,128)S(1)}, f32[3,1,4,4,4,128]{5,4,3,2,1,0:T(4,128)S(1)}, u32[]{:S(2)}, u32[]{:S(2)}) collective-permute-start(f32[3,1,4,4,4,128]{5,4,3,2,1,0:T(4,128)S(1)} %pad_maximum_fusion.3), channel_id=1, source_target_pairs={{0,1},{1,2},{2,3},{3,4},{4,5},{5,6},{6,7},{8,9},{9,10},{10,11},{11... | collective-permute-start | bytes 294920 | tf_op jit(solution)/shard_map/ppermute | solution.py:18
  309.3 2.2 collective-permute-done.30
  312.2 8.8 %fusion.43 = f32[1,1,8,4,128]{4,3,2,1,0:T(4,128)} fusion(f32[8,4,128]{2,1,0:T(4,128)S(1)} %get-tuple-element.20, f32[8,14,4,128]{3,2,1,0:T(4,128)S(1)} %bitcast.435, f32[1,1,8,14,128,128]{5,4,3,2,1,0:T(8,128)} %param.16, f32[1,1,8,4,128]{4,3,2,1,0:T(4,128)S(1)} %copy-done.3, f32[8,128]{1,0:T(8,128)S(1)} %bitcast.465), kind=kOutput, calls=%fused_computation.43 | convolution fusion | flops 88104960 | bytes 7622656 | tf_op jit(solution)/shard_map/bkij,bkrj->bri/dot_general | solution.py:35
  (161 shorter events, 53.1 us)
Async XLA Ops:
  3.1 7.2 %collective-permute-start.1 = (f32[1,1,4,4,4,128]{5,4,3,2,1,0:T(4,128)S(1)}, f32[1,1,4,4,4,128]{5,4,3,2,1,0:T(4,128)S(1)}, u32[]{:S(2)}, u32[]{:S(2)}) collective-permute-start(f32[1,1,4,4,4,128]{5,4,3,2,1,0:T(4,128)S(1)} %bitcast.449), channel_id=1, source_target_pairs={{8,0},{16,8},{24,16},{9,1},{17,9},{25,17},{10,2},{18,10},{26,18},{... | collective-permute-start | bytes 98312 | tf_op jit(solution)/shard_map/ppermute | solution.py:19
  5.1 5.5 %collective-permute-start = (f32[1,1,4,4,4,128]{5,4,3,2,1,0:T(4,128)S(1)}, f32[1,1,4,4,4,128]{5,4,3,2,1,0:T(4,128)S(1)}, u32[]{:S(2)}, u32[]{:S(2)}) collective-permute-start(f32[1,1,4,4,4,128]{5,4,3,2,1,0:T(4,128)S(1)} %bitcast.450), channel_id=1, source_target_pairs={{0,8},{8,16},{16,24},{1,9},{9,17},{17,25},{2,10},{10,18},{18,26},{... | collective-permute-start | bytes 98312 | tf_op jit(solution)/shard_map/ppermute | solution.py:18
  10.6 8.5 %collective-permute-start.3 = (f32[3,1,4,4,4,128]{5,4,3,2,1,0:T(4,128)S(1)}, f32[3,1,4,4,4,128]{5,4,3,2,1,0:T(4,128)S(1)}, u32[]{:S(2)}, u32[]{:S(2)}) collective-permute-start(f32[3,1,4,4,4,128]{5,4,3,2,1,0:T(4,128)S(1)} %pad_maximum_fusion), channel_id=1, source_target_pairs={{1,0},{2,1},{3,2},{4,3},{5,4},{6,5},{7,6},{9,8},{10,9},{11,10},{12... | collective-permute-start | bytes 294920 | tf_op jit(solution)/shard_map/ppermute | solution.py:19
  11.9 7.2 %collective-permute-start.2 = (f32[3,1,4,4,4,128]{5,4,3,2,1,0:T(4,128)S(1)}, f32[3,1,4,4,4,128]{5,4,3,2,1,0:T(4,128)S(1)}, u32[]{:S(2)}, u32[]{:S(2)}) collective-permute-start(f32[3,1,4,4,4,128]{5,4,3,2,1,0:T(4,128)S(1)} %pad_maximum_fusion), channel_id=1, source_target_pairs={{0,1},{1,2},{2,3},{3,4},{4,5},{5,6},{6,7},{8,9},{9,10},{10,11},{11... | collective-permute-start | bytes 294920 | tf_op jit(solution)/shard_map/ppermute | solution.py:18
  28.8 5.8 %collective-permute-start.5 = (f32[1,1,4,4,4,128]{5,4,3,2,1,0:T(4,128)S(1)}, f32[1,1,4,4,4,128]{5,4,3,2,1,0:T(4,128)S(1)}, u32[]{:S(2)}, u32[]{:S(2)}) collective-permute-start(f32[1,1,4,4,4,128]{5,4,3,2,1,0:T(4,128)S(1)} %bitcast.452), channel_id=1, source_target_pairs={{8,0},{16,8},{24,16},{9,1},{17,9},{25,17},{10,2},{18,10},{26,18},{... | collective-permute-start | bytes 98312 | tf_op jit(solution)/shard_map/ppermute | solution.py:19
  31.0 4.5 %collective-permute-start.4 = (f32[1,1,4,4,4,128]{5,4,3,2,1,0:T(4,128)S(1)}, f32[1,1,4,4,4,128]{5,4,3,2,1,0:T(4,128)S(1)}, u32[]{:S(2)}, u32[]{:S(2)}) collective-permute-start(f32[1,1,4,4,4,128]{5,4,3,2,1,0:T(4,128)S(1)} %bitcast.453), channel_id=1, source_target_pairs={{0,8},{8,16},{16,24},{1,9},{9,17},{17,25},{2,10},{10,18},{18,26},{... | collective-permute-start | bytes 98312 | tf_op jit(solution)/shard_map/ppermute | solution.py:18
  35.5 9.1 %collective-permute-start.7 = (f32[3,1,4,4,4,128]{5,4,3,2,1,0:T(4,128)S(1)}, f32[3,1,4,4,4,128]{5,4,3,2,1,0:T(4,128)S(1)}, u32[]{:S(2)}, u32[]{:S(2)}) collective-permute-start(f32[3,1,4,4,4,128]{5,4,3,2,1,0:T(4,128)S(1)} %pad_maximum_fusion.1), channel_id=1, source_target_pairs={{1,0},{2,1},{3,2},{4,3},{5,4},{6,5},{7,6},{9,8},{10,9},{11,10},{12... | collective-permute-start | bytes 294920 | tf_op jit(solution)/shard_map/ppermute | solution.py:19
  37.0 7.6 %collective-permute-start.6 = (f32[3,1,4,4,4,128]{5,4,3,2,1,0:T(4,128)S(1)}, f32[3,1,4,4,4,128]{5,4,3,2,1,0:T(4,128)S(1)}, u32[]{:S(2)}, u32[]{:S(2)}) collective-permute-start(f32[3,1,4,4,4,128]{5,4,3,2,1,0:T(4,128)S(1)} %pad_maximum_fusion.1), channel_id=1, source_target_pairs={{0,1},{1,2},{2,3},{3,4},{4,5},{5,6},{6,7},{8,9},{9,10},{10,11},{11... | collective-permute-start | bytes 294920 | tf_op jit(solution)/shard_map/ppermute | solution.py:18
  54.9 6.0 %collective-permute-start.8 = (f32[1,1,4,2,4,128]{5,4,3,2,1,0:T(4,128)S(1)}, f32[1,1,4,2,4,128]{5,4,3,2,1,0:T(4,128)S(1)}, u32[]{:S(2)}, u32[]{:S(2)}) collective-permute-start(f32[1,1,4,2,4,128]{5,4,3,2,1,0:T(4,128)S(1)} %copy.90), channel_id=1, source_target_pairs={{0,8},{8,16},{16,24},{1,9},{9,17},{17,25},{2,10},{10,18},{18,26},{... | collective-permute-start | bytes 49160 | tf_op jit(solution)/shard_map/ppermute | solution.py:18
  59.0 5.1 %collective-permute-start.9 = (f32[1,1,4,2,4,128]{5,4,3,2,1,0:T(4,128)S(1)}, f32[1,1,4,2,4,128]{5,4,3,2,1,0:T(4,128)S(1)}, u32[]{:S(2)}, u32[]{:S(2)}) collective-permute-start(f32[1,1,4,2,4,128]{5,4,3,2,1,0:T(4,128)S(1)} %copy.90), channel_id=1, source_target_pairs={{8,0},{16,8},{24,16},{9,1},{17,9},{25,17},{10,2},{18,10},{26,18},{... | collective-permute-start | bytes 49160 | tf_op jit(solution)/shard_map/ppermute | solution.py:19
  64.1 7.7 %collective-permute-start.11 = (f32[3,1,4,2,4,128]{5,4,3,2,1,0:T(4,128)S(1)}, f32[3,1,4,2,4,128]{5,4,3,2,1,0:T(4,128)S(1)}, u32[]{:S(2)}, u32[]{:S(2)}) collective-permute-start(f32[3,1,4,2,4,128]{5,4,3,2,1,0:T(4,128)S(1)} %constant_dynamic-update-slice_fusion.10), channel_id=1, source_target_pairs={{1,0},{2,1},{3,2},{4,3},{5,4},{6,5},{7,6},{9,8},{10,9},{11,10},{12... | collective-permute-start | bytes 147464 | tf_op jit(solution)/shard_map/ppermute | solution.py:19
  65.3 6.4 %collective-permute-start.10 = (f32[3,1,4,2,4,128]{5,4,3,2,1,0:T(4,128)S(1)}, f32[3,1,4,2,4,128]{5,4,3,2,1,0:T(4,128)S(1)}, u32[]{:S(2)}, u32[]{:S(2)}) collective-permute-start(f32[3,1,4,2,4,128]{5,4,3,2,1,0:T(4,128)S(1)} %constant_dynamic-update-slice_fusion.10), channel_id=1, source_target_pairs={{0,1},{1,2},{2,3},{3,4},{4,5},{5,6},{6,7},{8,9},{9,10},{10,11},{11... | collective-permute-start | bytes 147464 | tf_op jit(solution)/shard_map/ppermute | solution.py:18
  74.6 4.7 %collective-permute-start.12 = (f32[1,1,4,2,4,128]{5,4,3,2,1,0:T(4,128)S(1)}, f32[1,1,4,2,4,128]{5,4,3,2,1,0:T(4,128)S(1)}, u32[]{:S(2)}, u32[]{:S(2)}) collective-permute-start(f32[1,1,4,2,4,128]{5,4,3,2,1,0:T(4,128)S(1)} %copy.95), channel_id=1, source_target_pairs={{0,8},{8,16},{16,24},{1,9},{9,17},{17,25},{2,10},{10,18},{18,26},{... | collective-permute-start | bytes 49160 | tf_op jit(solution)/shard_map/ppermute | solution.py:18
  77.4 5.1 %collective-permute-start.13 = (f32[1,1,4,2,4,128]{5,4,3,2,1,0:T(4,128)S(1)}, f32[1,1,4,2,4,128]{5,4,3,2,1,0:T(4,128)S(1)}, u32[]{:S(2)}, u32[]{:S(2)}) collective-permute-start(f32[1,1,4,2,4,128]{5,4,3,2,1,0:T(4,128)S(1)} %copy.95), channel_id=1, source_target_pairs={{8,0},{16,8},{24,16},{9,1},{17,9},{25,17},{10,2},{18,10},{26,18},{... | collective-permute-start | bytes 49160 | tf_op jit(solution)/shard_map/ppermute | solution.py:19
  82.5 8.0 %collective-permute-start.15 = (f32[3,1,4,2,4,128]{5,4,3,2,1,0:T(4,128)S(1)}, f32[3,1,4,2,4,128]{5,4,3,2,1,0:T(4,128)S(1)}, u32[]{:S(2)}, u32[]{:S(2)}) collective-permute-start(f32[3,1,4,2,4,128]{5,4,3,2,1,0:T(4,128)S(1)} %constant_dynamic-update-slice_fusion.18), channel_id=1, source_target_pairs={{1,0},{2,1},{3,2},{4,3},{5,4},{6,5},{7,6},{9,8},{10,9},{11,10},{12... | collective-permute-start | bytes 147464 | tf_op jit(solution)/shard_map/ppermute | solution.py:19
  83.7 6.7 %collective-permute-start.14 = (f32[3,1,4,2,4,128]{5,4,3,2,1,0:T(4,128)S(1)}, f32[3,1,4,2,4,128]{5,4,3,2,1,0:T(4,128)S(1)}, u32[]{:S(2)}, u32[]{:S(2)}) collective-permute-start(f32[3,1,4,2,4,128]{5,4,3,2,1,0:T(4,128)S(1)} %constant_dynamic-update-slice_fusion.18), channel_id=1, source_target_pairs={{0,1},{1,2},{2,3},{3,4},{4,5},{5,6},{6,7},{8,9},{9,10},{10,11},{11... | collective-permute-start | bytes 147464 | tf_op jit(solution)/shard_map/ppermute | solution.py:18
  221.8 15.9 %collective-permute-start.16 = (f32[1,1,4,2,4,128]{5,4,3,2,1,0:T(4,128)S(1)}, f32[1,1,4,2,4,128]{5,4,3,2,1,0:T(4,128)S(1)}, u32[]{:S(2)}, u32[]{:S(2)}) collective-permute-start(f32[1,1,4,2,4,128]{5,4,3,2,1,0:T(4,128)S(1)} %copy.103), channel_id=1, source_target_pairs={{0,8},{8,16},{16,24},{1,9},{9,17},{17,25},{2,10},{10,18},{18,26},{... | collective-permute-start | bytes 49160 | tf_op jit(solution)/shard_map/ppermute | solution.py:18
  235.7 5.1 %collective-permute-start.17 = (f32[1,1,4,2,4,128]{5,4,3,2,1,0:T(4,128)S(1)}, f32[1,1,4,2,4,128]{5,4,3,2,1,0:T(4,128)S(1)}, u32[]{:S(2)}, u32[]{:S(2)}) collective-permute-start(f32[1,1,4,2,4,128]{5,4,3,2,1,0:T(4,128)S(1)} %copy.103), channel_id=1, source_target_pairs={{8,0},{16,8},{24,16},{9,1},{17,9},{25,17},{10,2},{18,10},{26,18},{... | collective-permute-start | bytes 49160 | tf_op jit(solution)/shard_map/ppermute | solution.py:19
  240.8 7.0 %collective-permute-start.19 = (f32[3,1,4,2,4,128]{5,4,3,2,1,0:T(4,128)S(1)}, f32[3,1,4,2,4,128]{5,4,3,2,1,0:T(4,128)S(1)}, u32[]{:S(2)}, u32[]{:S(2)}) collective-permute-start(f32[3,1,4,2,4,128]{5,4,3,2,1,0:T(4,128)S(1)} %constant_dynamic-update-slice_fusion.26), channel_id=1, source_target_pairs={{1,0},{2,1},{3,2},{4,3},{5,4},{6,5},{7,6},{9,8},{10,9},{11,10},{12... | collective-permute-start | bytes 147464 | tf_op jit(solution)/shard_map/ppermute | solution.py:19
  242.1 5.7 %collective-permute-start.18 = (f32[3,1,4,2,4,128]{5,4,3,2,1,0:T(4,128)S(1)}, f32[3,1,4,2,4,128]{5,4,3,2,1,0:T(4,128)S(1)}, u32[]{:S(2)}, u32[]{:S(2)}) collective-permute-start(f32[3,1,4,2,4,128]{5,4,3,2,1,0:T(4,128)S(1)} %constant_dynamic-update-slice_fusion.26), channel_id=1, source_target_pairs={{0,1},{1,2},{2,3},{3,4},{4,5},{5,6},{6,7},{8,9},{9,10},{10,11},{11... | collective-permute-start | bytes 147464 | tf_op jit(solution)/shard_map/ppermute | solution.py:18
  250.6 4.7 %collective-permute-start.20 = (f32[1,1,4,2,4,128]{5,4,3,2,1,0:T(4,128)S(1)}, f32[1,1,4,2,4,128]{5,4,3,2,1,0:T(4,128)S(1)}, u32[]{:S(2)}, u32[]{:S(2)}) collective-permute-start(f32[1,1,4,2,4,128]{5,4,3,2,1,0:T(4,128)S(1)} %copy.108), channel_id=1, source_target_pairs={{0,8},{8,16},{16,24},{1,9},{9,17},{17,25},{2,10},{10,18},{18,26},{... | collective-permute-start | bytes 49160 | tf_op jit(solution)/shard_map/ppermute | solution.py:18
  253.4 5.1 %collective-permute-start.21 = (f32[1,1,4,2,4,128]{5,4,3,2,1,0:T(4,128)S(1)}, f32[1,1,4,2,4,128]{5,4,3,2,1,0:T(4,128)S(1)}, u32[]{:S(2)}, u32[]{:S(2)}) collective-permute-start(f32[1,1,4,2,4,128]{5,4,3,2,1,0:T(4,128)S(1)} %copy.108), channel_id=1, source_target_pairs={{8,0},{16,8},{24,16},{9,1},{17,9},{25,17},{10,2},{18,10},{26,18},{... | collective-permute-start | bytes 49160 | tf_op jit(solution)/shard_map/ppermute | solution.py:19
  258.5 7.6 %collective-permute-start.23 = (f32[3,1,4,2,4,128]{5,4,3,2,1,0:T(4,128)S(1)}, f32[3,1,4,2,4,128]{5,4,3,2,1,0:T(4,128)S(1)}, u32[]{:S(2)}, u32[]{:S(2)}) collective-permute-start(f32[3,1,4,2,4,128]{5,4,3,2,1,0:T(4,128)S(1)} %constant_dynamic-update-slice_fusion.34), channel_id=1, source_target_pairs={{1,0},{2,1},{3,2},{4,3},{5,4},{6,5},{7,6},{9,8},{10,9},{11,10},{12... | collective-permute-start | bytes 147464 | tf_op jit(solution)/shard_map/ppermute | solution.py:19
  259.8 6.3 %collective-permute-start.22 = (f32[3,1,4,2,4,128]{5,4,3,2,1,0:T(4,128)S(1)}, f32[3,1,4,2,4,128]{5,4,3,2,1,0:T(4,128)S(1)}, u32[]{:S(2)}, u32[]{:S(2)}) collective-permute-start(f32[3,1,4,2,4,128]{5,4,3,2,1,0:T(4,128)S(1)} %constant_dynamic-update-slice_fusion.34), channel_id=1, source_target_pairs={{0,1},{1,2},{2,3},{3,4},{4,5},{5,6},{6,7},{8,9},{9,10},{10,11},{11... | collective-permute-start | bytes 147464 | tf_op jit(solution)/shard_map/ppermute | solution.py:18
  270.1 5.6 %collective-permute-start.25 = (f32[1,1,4,4,4,128]{5,4,3,2,1,0:T(4,128)S(1)}, f32[1,1,4,4,4,128]{5,4,3,2,1,0:T(4,128)S(1)}, u32[]{:S(2)}, u32[]{:S(2)}) collective-permute-start(f32[1,1,4,4,4,128]{5,4,3,2,1,0:T(4,128)S(1)} %bitcast.458), channel_id=1, source_target_pairs={{8,0},{16,8},{24,16},{9,1},{17,9},{25,17},{10,2},{18,10},{26,18},{... | collective-permute-start | bytes 98312 | tf_op jit(solution)/shard_map/ppermute | solution.py:19
  272.0 4.7 %collective-permute-start.24 = (f32[1,1,4,4,4,128]{5,4,3,2,1,0:T(4,128)S(1)}, f32[1,1,4,4,4,128]{5,4,3,2,1,0:T(4,128)S(1)}, u32[]{:S(2)}, u32[]{:S(2)}) collective-permute-start(f32[1,1,4,4,4,128]{5,4,3,2,1,0:T(4,128)S(1)} %bitcast.459), channel_id=1, source_target_pairs={{0,8},{8,16},{16,24},{1,9},{9,17},{17,25},{2,10},{10,18},{18,26},{... | collective-permute-start | bytes 98312 | tf_op jit(solution)/shard_map/ppermute | solution.py:18
  276.7 9.7 %collective-permute-start.27 = (f32[3,1,4,4,4,128]{5,4,3,2,1,0:T(4,128)S(1)}, f32[3,1,4,4,4,128]{5,4,3,2,1,0:T(4,128)S(1)}, u32[]{:S(2)}, u32[]{:S(2)}) collective-permute-start(f32[3,1,4,4,4,128]{5,4,3,2,1,0:T(4,128)S(1)} %pad_maximum_fusion.2), channel_id=1, source_target_pairs={{1,0},{2,1},{3,2},{4,3},{5,4},{6,5},{7,6},{9,8},{10,9},{11,10},{12... | collective-permute-start | bytes 294920 | tf_op jit(solution)/shard_map/ppermute | solution.py:19
  278.0 8.3 %collective-permute-start.26 = (f32[3,1,4,4,4,128]{5,4,3,2,1,0:T(4,128)S(1)}, f32[3,1,4,4,4,128]{5,4,3,2,1,0:T(4,128)S(1)}, u32[]{:S(2)}, u32[]{:S(2)}) collective-permute-start(f32[3,1,4,4,4,128]{5,4,3,2,1,0:T(4,128)S(1)} %pad_maximum_fusion.2), channel_id=1, source_target_pairs={{0,1},{1,2},{2,3},{3,4},{4,5},{5,6},{6,7},{8,9},{9,10},{10,11},{11... | collective-permute-start | bytes 294920 | tf_op jit(solution)/shard_map/ppermute | solution.py:18
  295.9 5.8 %collective-permute-start.29 = (f32[1,1,4,4,4,128]{5,4,3,2,1,0:T(4,128)S(1)}, f32[1,1,4,4,4,128]{5,4,3,2,1,0:T(4,128)S(1)}, u32[]{:S(2)}, u32[]{:S(2)}) collective-permute-start(f32[1,1,4,4,4,128]{5,4,3,2,1,0:T(4,128)S(1)} %bitcast.455), channel_id=1, source_target_pairs={{8,0},{16,8},{24,16},{9,1},{17,9},{25,17},{10,2},{18,10},{26,18},{... | collective-permute-start | bytes 98312 | tf_op jit(solution)/shard_map/ppermute | solution.py:19
  298.0 4.7 %collective-permute-start.28 = (f32[1,1,4,4,4,128]{5,4,3,2,1,0:T(4,128)S(1)}, f32[1,1,4,4,4,128]{5,4,3,2,1,0:T(4,128)S(1)}, u32[]{:S(2)}, u32[]{:S(2)}) collective-permute-start(f32[1,1,4,4,4,128]{5,4,3,2,1,0:T(4,128)S(1)} %bitcast.456), channel_id=1, source_target_pairs={{0,8},{8,16},{16,24},{1,9},{9,17},{17,25},{2,10},{10,18},{18,26},{... | collective-permute-start | bytes 98312 | tf_op jit(solution)/shard_map/ppermute | solution.py:18
  302.7 8.7 %collective-permute-start.31 = (f32[3,1,4,4,4,128]{5,4,3,2,1,0:T(4,128)S(1)}, f32[3,1,4,4,4,128]{5,4,3,2,1,0:T(4,128)S(1)}, u32[]{:S(2)}, u32[]{:S(2)}) collective-permute-start(f32[3,1,4,4,4,128]{5,4,3,2,1,0:T(4,128)S(1)} %pad_maximum_fusion.3), channel_id=1, source_target_pairs={{1,0},{2,1},{3,2},{4,3},{5,4},{6,5},{7,6},{9,8},{10,9},{11,10},{12... | collective-permute-start | bytes 294920 | tf_op jit(solution)/shard_map/ppermute | solution.py:19
  304.0 7.4 %collective-permute-start.30 = (f32[3,1,4,4,4,128]{5,4,3,2,1,0:T(4,128)S(1)}, f32[3,1,4,4,4,128]{5,4,3,2,1,0:T(4,128)S(1)}, u32[]{:S(2)}, u32[]{:S(2)}) collective-permute-start(f32[3,1,4,4,4,128]{5,4,3,2,1,0:T(4,128)S(1)} %pad_maximum_fusion.3), channel_id=1, source_target_pairs={{0,1},{1,2},{2,3},{3,4},{4,5},{5,6},{6,7},{8,9},{9,10},{10,11},{11... | collective-permute-start | bytes 294920 | tf_op jit(solution)/shard_map/ppermute | solution.py:18
  (10 other events, 553.3 us)
